TPU v7x, 16 devices: a whole 2x2x2 slice. The times are simulated.
16 devices in a mesh: dp: 4 (over z, y), tp: 4 (over x, core).
Axes of the slice: x: 2, y: 2, z: 2, core: 2. Of those that a mesh axis runs over, the one named last changes fastest.
Arguments:
- x_in: bfloat16 [1024, 4096], P(('dp', 'tp')), parts along dimension 0
- w_in: bfloat16 [4096, 16384], P(None, 'tp')
- grad_out: bfloat16 [1024, 16384], P('dp', 'tp'), parts along dimension 0
Outputs:
- output 1: bfloat16 [1024, 4096], P(('dp', 'tp')), parts along dimension 0
- output 2: float32 [16384, 16384], P('dp', 'tp'), parts along dimension 0
There are 4 independent parts. A program takes and returns all parts, laid end to end along the dimension named above; an argument that names none is the same for every part.
All inputs are finite; a program needn't handle non-finite values.
Results may differ from a plain program's by a relative error of at most 0.001.
Values are sent between devices in bfloat16 or wider.
A program may use at most 1 GiB of HBM per device.

v0:
```python
import jax
import jax.numpy as jnp
from jax import lax
from jax.sharding import PartitionSpec as P


def solution(mesh):
    def per_device(x_blk, w_blk, grad_blk):
        x_full = lax.all_gather(x_blk, "tp", axis=0, tiled=True)
        part_dx = lax.dot_general(grad_blk, w_blk, (((1,), (1,)), ((), ())), preferred_element_type=jnp.float32)
        grad_x = lax.psum_scatter(part_dx, "tp", scatter_dimension=0, tiled=True).astype(jnp.bfloat16)
        grad_w = lax.dot_general(x_full, grad_blk, (((0,), (0,)), ((), ())), preferred_element_type=jnp.float32)
        return grad_x, grad_w

    return jax.shard_map(
        per_device,
        mesh=mesh,
        in_specs=(P(("dp", "tp"), None), P(None, "tp"), P("dp", "tp")),
        out_specs=(P(("dp", "tp"), None), P("dp", "tp")),
        check_vma=False,
    )
```

profile of v0, /device:TPU:0, one launch (start us, length us, event | category | flops | bytes accessed | tf_op | source)
XLA Modules:
  0.0 85.3 jit_solution(11457767159491095508)
XLA Ops:
  7.2 0.0 copy-start
  7.2 0.0 all-gather.2.cloned.1.call-start
  7.2 0.7 all-gather.2.cloned.1.call-update
  7.9 0.0 reduce-scatter.2.cloned.1.call-start
  8.0 0.8 copy-done
  8.8 16.8 %fusion = f32[256,4096]{1,0:T(8,128)} fusion(bf16[256,4096]{1,0:T(8,128)(2,1)S(1)} %copy-done, bf16[4096,4096]{1,0:T(8,128)(2,1)} %param.4), kind=kOutput, calls=%fused_computation | convolution fusion | flops 8589934592 | bytes 39845888 | tf_op jit(solution)/shard_map/dot_general | solution.py:10
  25.6 0.0 reduce-scatter.2.cloned.1.call-update
  25.6 7.5 %all-gather.2.cloned.1.call-done = bf16[256,4096]{1,0:T(8,128)(2,1)} async-done(((bf16[64,4096]{1,0:T(8,128)(2,1)}), bf16[256,4096]{1,0:T(8,128)(2,1)}) %all-gather.2.cloned.1.call-update) | async-done | bytes 2097168 | tf_op jit(solution)/shard_map/all_gather | solution.py:9
  33.0 27.6 %fusion.1 = f32[4096,4096]{1,0:T(8,128)} fusion(bf16[256,4096]{1,0:T(8,128)(2,1)} %all-gather.2.cloned.1.call-done, bf16[256,4096]{1,0:T(8,128)(2,1)S(1)} %copy-done), kind=kOutput, calls=%fused_computation.1 | convolution fusion | flops 8589934592 | bytes 71303168 | tf_op jit(solution)/shard_map/dot_general | solution.py:12
  60.6 15.8 %reduce-scatter.2.cloned.1.call-done = f32[64,4096]{1,0:T(8,128)} async-done(((f32[256,4096]{1,0:T(8,128)}), f32[64,4096]{1,0:T(8,128)}) %reduce-scatter.2.cloned.1.call-update) | async-done | bytes 1048592 | tf_op jit(solution)/shard_map/reduce_scatter | solution.py:11
  76.4 2.1 %convert_element_type.3 = bf16[64,4096]{1,0:T(8,128)(2,1)} convert(f32[64,4096]{1,0:T(8,128)} %reduce-scatter.2.cloned.1.call-done) | non-fusion elementwise | flops 262144 | bytes 1572864 | tf_op jit(solution)/shard_map/convert_element_type | solution.py:11
Async XLA Ops:
  7.2 1.6 %copy-start = (bf16[256,4096]{1,0:T(8,128)(2,1)S(1)}, bf16[256,4096]{1,0:T(8,128)(2,1)}, u32[]{:S(2)}) copy-start(bf16[256,4096]{1,0:T(8,128)(2,1)} %param.5) | copy-start | bytes 6291460
  7.2 25.9 %all-gather.2.cloned.1.call-start = ((), (), s32[]{:S(2)}) async-start(), calls=%async_computation.2 | async-start | bytes 2621440 | tf_op jit(solution)/shard_map/all_gather | solution.py:9
  7.9 68.5 %reduce-scatter.2.cloned.1.call-start = ((), (), s32[]{:S(2)}) async-start(), calls=%async_computation.1 | async-start | bytes 5242880 | tf_op jit(solution)/shard_map/reduce_scatter | solution.py:11
Sparse Core Ops, SparseCore 0:
  9.5 23.4 all-gather.1
  35.5 40.8 reduce-scatter.1
where the time goes:
time: 85.6 us; the launch traced here: 85.3 us
  matrix products  44.3 us (52%)
  waiting for transfers between devices  24 us (28%)
  between operations  14 us (16%)
  other arithmetic  2.07 us (2%)
    dot_general x1, matrix products, per_device(): lax.dot_general(x_full, grad_blk, (((0,), (0,)), ((), ())), preferred_ele...  27.6 us
    dot_general x1, matrix products, per_device(): lax.dot_general(grad_blk, w_blk, (((1,), (1,)), ((), ())), preferred_elem...  16.8 us
    reduce_scatter x1, waiting for transfers between devices, per_device(): lax.psum_scatter(part_dx, 'tp', scatter_dimension=0, tiled=True)  15.8 us
    all_gather x1, waiting for transfers between devices, per_device(): x_full = lax.all_gather(x_blk, 'tp', axis=0, tiled=True)  7.46 us
    convert_element_type x1, other arithmetic, per_device(): lax.psum_scatter(part_dx, 'tp', scatter_dimension=0, tiled=True)  2.07 us
  transfers between devices with their start and end apart: 2, of which 2 were waited for; matrix products, arithmetic and copies ran while one was open for 52% of the time, Pallas kernels for 0%

commit v1 on v0

v1 whole, which is shorter than its diff:
```python
import functools

import jax
import jax.numpy as jnp
from jax import lax
from jax.experimental import pallas as pl
from jax.experimental.pallas import tpu as pltpu
from jax.sharding import PartitionSpec as P


MESH = pl.DeviceIdType.MESH
CROSS = [(0, 2), (1, 3), (2, 0), (3, 1)]
SIBLING = [(0, 1), (1, 0), (2, 3), (3, 2)]


def neighbours():
    me = lax.axis_index("tp")
    sib = me + 1 - 2 * lax.rem(me, 2)
    return me, lax.rem(me + 2, 4), sib, lax.rem(sib + 2, 4)


def dx_kernel(chunk, depth, g_ref, w_ref, far_ref, near_ref, g_buf, w_buf, own, send, recv, out_buf,
              g_sem, w_sem, send_sem, recv_sem, out_sem):
    order = neighbours()
    sib = order[2]
    tokens = g_ref.shape[0] // 4
    steps = w_ref.shape[0] // chunk

    def fetch_w(c):
        slot = lax.rem(c, depth)
        rows = pl.ds(pl.multiple_of(c * chunk, chunk), chunk)
        return pltpu.make_async_copy(w_ref.at[rows], w_buf.at[slot], w_sem.at[slot])

    g_copies = []
    for j, idx in enumerate(order):
        rows = pl.ds(pl.multiple_of(idx * tokens, tokens), tokens)
        g_copies.append(pltpu.make_async_copy(g_ref.at[rows], g_buf.at[pl.ds(j * tokens, tokens)], g_sem.at[j]))
        g_copies[-1].start()
    for c in range(depth):
        fetch_w(c).start()

    barrier = pltpu.get_barrier_semaphore()
    pl.semaphore_signal(barrier, inc=1, device_id={"tp": sib}, device_id_type=MESH)
    pl.semaphore_wait(barrier, 1)
    for copy in g_copies:
        copy.wait()

    def to_sibling(c):
        return pltpu.make_async_remote_copy(
            src_ref=send.at[c], dst_ref=recv.at[c], send_sem=send_sem.at[c], recv_sem=recv_sem.at[c],
            device_id={"tp": sib}, device_id_type=MESH)

    def put(c, half, ref):
        cols = pl.ds(pl.multiple_of(c * chunk, chunk), chunk)
        return pltpu.make_async_copy(
            out_buf.at[c, pl.ds(half * tokens, tokens)], ref.at[:, cols], out_sem.at[half, c])

    def finish(c):
        to_sibling(c).wait_recv()
        out_buf[c] = own[c] + recv[c]
        put(c, 1, far_ref).start()
        put(c, 0, near_ref).start()

    def step(c, carry):
        fetch_w(c).wait()
        part = lax.dot_general(g_buf[...], w_buf[lax.rem(c, depth)], (((1,), (1,)), ((), ())),
                               preferred_element_type=jnp.float32)
        own[c] = part[: 2 * tokens]
        send[c] = part[2 * tokens:]

        @pl.when(c + depth < steps)
        def _():
            fetch_w(c + depth).start()

        @pl.when(c >= 1)
        def _():
            finish(c - 1)

        to_sibling(c).start()
        return carry

    lax.fori_loop(0, steps, step, 0)
    finish(steps - 1)

    def drain(c, carry):
        to_sibling(c).wait_send()
        put(c, 0, near_ref).wait()
        put(c, 1, far_ref).wait()
        return carry

    lax.fori_loop(0, steps, drain, 0)


def dx_partial(g, w, chunk=512, depth=3):
    tokens, (hidden, ffn) = g.shape[0] // 4, w.shape
    steps = hidden // chunk
    piece = jax.ShapeDtypeStruct((tokens, hidden), jnp.float32)
    return pl.pallas_call(
        functools.partial(dx_kernel, chunk, depth),
        out_shape=(piece, piece),
        in_specs=[pl.BlockSpec(memory_space=pl.ANY)] * 2,
        out_specs=[pl.BlockSpec(memory_space=pl.ANY)] * 2,
        scratch_shapes=[
            pltpu.VMEM(g.shape, g.dtype),
            pltpu.VMEM((depth, chunk, ffn), w.dtype),
            pltpu.VMEM((steps, 2 * tokens, chunk), jnp.float32),
            pltpu.VMEM((steps, 2 * tokens, chunk), jnp.float32),
            pltpu.VMEM((steps, 2 * tokens, chunk), jnp.float32),
            pltpu.VMEM((steps, 2 * tokens, chunk), jnp.float32),
            pltpu.SemaphoreType.DMA((4,)),
            pltpu.SemaphoreType.DMA((depth,)),
            pltpu.SemaphoreType.DMA((steps,)),
            pltpu.SemaphoreType.DMA((steps,)),
            pltpu.SemaphoreType.DMA((2, steps)),
        ],
        cost_estimate=pl.CostEstimate(
            flops=2 * g.shape[0] * hidden * ffn, bytes_accessed=2 * hidden * ffn, transcendentals=0),
        compiler_params=pltpu.CompilerParams(
            collective_id=0, has_side_effects=True, vmem_limit_bytes=40 * 1024 * 1024),
        name="dx_partial",
    )(g, w)


def dw_kernel(x0, x1, x2, x3, g_ref, out_ref, x_buf):
    tokens = x0.shape[0]
    for idx, x in zip(neighbours(), (x0, x1, x2, x3)):
        x_buf[pl.ds(pl.multiple_of(idx * tokens, tokens), tokens), :] = x[...]
    out_ref[...] = lax.dot_general(x_buf[...], g_ref[...], (((0,), (0,)), ((), ())),
                                   preferred_element_type=jnp.float32)


def dw(blocks, g, rows=256):
    tokens, hidden = blocks[0].shape
    ffn = g.shape[1]
    return pl.pallas_call(
        dw_kernel,
        out_shape=jax.ShapeDtypeStruct((hidden, ffn), jnp.float32),
        grid=(hidden // rows,),
        in_specs=[pl.BlockSpec((tokens, rows), lambda i: (0, i))] * 4
        + [pl.BlockSpec(g.shape, lambda i: (0, 0))],
        out_specs=pl.BlockSpec((rows, ffn), lambda i: (i, 0)),
        scratch_shapes=[pltpu.VMEM((4 * tokens, rows), g.dtype)],
        cost_estimate=pl.CostEstimate(
            flops=8 * tokens * hidden * ffn, bytes_accessed=4 * hidden * ffn, transcendentals=0),
        compiler_params=pltpu.CompilerParams(vmem_limit_bytes=40 * 1024 * 1024),
        name="dw",
    )(*blocks, g)


def solution(mesh):
    def per_device(x, w, g):
        x_cross = lax.ppermute(x, "tp", CROSS)
        x_sib = lax.ppermute(x, "tp", SIBLING)
        far, near = dx_partial(g, w)
        arrived = lax.ppermute(far, "tp", CROSS)
        x_last = lax.ppermute(x_cross, "tp", SIBLING)
        grad_w = dw((x, x_cross, x_sib, x_last), g)
        return (near + arrived).astype(jnp.bfloat16), grad_w

    return jax.shard_map(
        per_device,
        mesh=mesh,
        in_specs=(P(("dp", "tp"), None), P(None, "tp"), P("dp", "tp")),
        out_specs=(P(("dp", "tp"), None), P("dp", "tp")),
        check_vma=False,
    )
```

time: 85.6 us -> 81.1 us (0.947)
  matrix products: 44.3 us -> 0 us
  Pallas kernels: 0 us -> 39.2 us
  between operations: 14 us -> 0.65 us
  waiting for transfers between devices: 24 us -> 35.8 us
  starting transfers between devices: 0.08 us -> 2.81 us
  other arithmetic: 2.07 us -> 0.89 us
    dot_general x2 -> x0, matrix products: 44.3 us -> none  [the longest x1 27.6 us: per_device(): lax.dot_general(x_full, grad_blk, (((0,), (0,)), ((), ())), preferred_ele...]
    pallas_call x0 -> x2, Pallas kernels: none -> 39.2 us  [the longest x1 23.7 us: dw(): pl.pallas_call(dw_kernel, out_shape=jax.ShapeDtypeStruct((hidden, ffn), j...]
    ppermute x0 -> x4, waiting for transfers between devices: none -> 35.8 us  [the longest x1 34.8 us: per_device(): x_cross = lax.ppermute(x, 'tp', CROSS)]
    reduce_scatter x1 -> x0, waiting for transfers between devices: 15.8 us -> none  [per_device(): lax.psum_scatter(part_dx, 'tp', scatter_dimension=0, tiled=True)]
    all_gather x1 -> x0, waiting for transfers between devices: 7.46 us -> none  [per_device(): x_full = lax.all_gather(x_blk, 'tp', axis=0, tiled=True)]
    ppermute x0 -> x4, starting transfers between devices: none -> 2.81 us  [the longest x1 2.75 us: per_device(): arrived = lax.ppermute(far, 'tp', CROSS)]
    convert_element_type x1, other arithmetic: 2.07 us -> 0.89 us  [per_device(): return ((near + arrived).astype(jnp.bfloat16), grad_w)]
  transfers between devices with their start and end apart: 2 -> 4, of which waited for: 2 -> 2; matrix products, arithmetic and copies ran while one was open for 52% -> 1% of each run, Pallas kernels for 0% -> 0%
where the time goes in v1:
time: 81.1 us; the launch traced here: 81 us
  Pallas kernels  39.2 us (48%)
  waiting for transfers between devices  35.8 us (44%)
  starting transfers between devices  2.81 us (3%)
  local copies, waits for them, and re-layouts  1.59 us (2%)
  other arithmetic  0.89 us (1%)
    ppermute x1, waiting for transfers between devices, per_device(): x_cross = lax.ppermute(x, 'tp', CROSS)  34.8 us
    pallas_call x1, Pallas kernels, dw(): pl.pallas_call(dw_kernel, out_shape=jax.ShapeDtypeStruct((hidden, ffn), j...  23.7 us
    pallas_call x1, Pallas kernels, dx_partial(): pl.pallas_call(functools.partial(dx_kernel, chunk, depth), out_shape=(pie...  15.5 us
    ppermute x1, starting transfers between devices, per_device(): arrived = lax.ppermute(far, 'tp', CROSS)  2.75 us
  transfers between devices with their start and end apart: 4, of which 2 were waited for; matrix products, arithmetic and copies ran while one was open for 1% of the time, Pallas kernels for 0%

profile of v1, /device:TPU:0, one launch (start us, length us, event | category | flops | bytes accessed | tf_op | source)
XLA Modules:
  0.0 81.0 jit_solution(10516464576677199438)
XLA Ops:
  0.6 0.0 copy-start
  0.6 1.6 %copy-done = bf16[256,4096]{1,0:T(8,128)(2,1)S(1)} copy-done((bf16[256,4096]{1,0:T(8,128)(2,1)S(1)}, bf16[256,4096]{1,0:T(8,128)(2,1)}, u32[]{:S(2)}) %copy-start) | copy-done | bytes 2097176
  2.2 0.0 copy-start.1
  2.2 15.5 %dx_partial.1 = (f32[64,4096]{1,0:T(8,128)S(1)}, f32[64,4096]{1,0:T(8,128)S(1)}) custom-call(bf16[256,4096]{1,0:T(8,128)(2,1)S(1)} %copy-done, bf16[4096,4096]{1,0:T(8,128)(2,1)} %w_ref.1), custom_call_target="tpu_custom_call" | custom-call | flops 8589934592 | bytes 33554432 | tf_op jit(solution)/shard_map/dx_partial/pallas_call | solution.py:98
  17.7 2.8 %collective-permute-start = (f32[64,4096]{1,0:T(8,128)S(1)}, f32[64,4096]{1,0:T(8,128)S(1)}, u32[]{:S(2)}, u32[]{:S(2)}) collective-permute-start(f32[64,4096]{1,0:T(8,128)S(1)} %get-tuple-element.5), channel_id=1, source_target_pairs={{0,2},{1,3},{2,0},{3,1},{4,6},{5,7},{6,4},{7,5},{8,10},{9,11},{10,... | collective-permute-start | bytes 3145736 | tf_op jit(solution)/shard_map/ppermute | solution.py:155
  20.5 0.0 copy-done.1
  20.5 0.1 collective-permute-start.1
  20.6 0.0 collective-permute-start.2
  20.6 34.8 %collective-permute-done.1.x1 = bf16[64,4096]{1,0:T(8,128)(2,1)S(1)} collective-permute-done((bf16[64,4096]{1,0:T(8,128)(2,1)S(1)}, bf16[64,4096]{1,0:T(8,128)(2,1)S(1)}, u32[]{:S(2)}, u32[]{:S(2)}) %collective-permute-start.1) | collective-permute-done | bytes 524320 | tf_op jit(solution)/shard_map/ppermute | solution.py:152
  55.3 0.0 collective-permute-start.3
  55.3 0.0 collective-permute-done
  55.3 0.9 %add_convert_fusion = bf16[64,4096]{1,0:T(8,128)(2,1)} fusion(f32[64,4096]{1,0:T(8,128)S(1)} %get-tuple-element.4, f32[64,4096]{1,0:T(8,128)S(1)} %collective-permute-done), kind=kLoop, calls=%fused_computation | loop fusion | flops 524288 | bytes 2621440 | tf_op jit(solution)/shard_map/convert_element_type | solution.py:158
  56.2 0.0 collective-permute-done.2.x2
  56.2 1.0 %collective-permute-done.3.x3 = bf16[64,4096]{1,0:T(8,128)(2,1)S(1)} collective-permute-done((bf16[64,4096]{1,0:T(8,128)(2,1)S(1)}, bf16[64,4096]{1,0:T(8,128)(2,1)S(1)}, u32[]{:S(2)}, u32[]{:S(2)}) %collective-permute-start.3) | collective-permute-done | bytes 524320 | tf_op jit(solution)/shard_map/ppermute | solution.py:156
  57.2 23.7 %dw.1 = f32[4096,4096]{1,0:T(8,128)} custom-call(bf16[64,4096]{1,0:T(8,128)(2,1)S(1)} %copy-done.1, bf16[64,4096]{1,0:T(8,128)(2,1)S(1)} %collective-permute-done.1.x1, bf16[64,4096]{1,0:T(8,128)(2,1)S(1)} %collective-permute-done.2.x2, bf16[64,4096]{1,0:T(8,128)(2,1)S(1)} %collective-permute-done.3.x3, bf16[256,4096]{1,0:T(8,128)(2,1)S(1)} %copy-done), custom_call_target="tpu_custom_call" | custom-call | flops 8589934592 | bytes 67108864 | tf_op jit(solution)/shard_map/dw/pallas_call | solution.py:135
Async XLA Ops:
  0.6 1.6 %copy-start = (bf16[256,4096]{1,0:T(8,128)(2,1)S(1)}, bf16[256,4096]{1,0:T(8,128)(2,1)}, u32[]{:S(2)}) copy-start(bf16[256,4096]{1,0:T(8,128)(2,1)} %g_ref.3) | copy-start | bytes 6291460
  2.2 18.3 %copy-start.1 = (bf16[64,4096]{1,0:T(8,128)(2,1)S(1)}, bf16[64,4096]{1,0:T(8,128)(2,1)}, u32[]{:S(2)}) copy-start(bf16[64,4096]{1,0:T(8,128)(2,1)} %x0.1) | copy-start | bytes 1572868
  17.7 37.6 %collective-permute-start = (f32[64,4096]{1,0:T(8,128)S(1)}, f32[64,4096]{1,0:T(8,128)S(1)}, u32[]{:S(2)}, u32[]{:S(2)}) collective-permute-start(f32[64,4096]{1,0:T(8,128)S(1)} %get-tuple-element.5), channel_id=1, source_target_pairs={{0,2},{1,3},{2,0},{3,1},{4,6},{5,7},{6,4},{7,5},{8,10},{9,11},{10,... | collective-permute-start | bytes 3145736 | tf_op jit(solution)/shard_map/ppermute | solution.py:155
  20.5 34.8 %collective-permute-start.1 = (bf16[64,4096]{1,0:T(8,128)(2,1)S(1)}, bf16[64,4096]{1,0:T(8,128)(2,1)S(1)}, u32[]{:S(2)}, u32[]{:S(2)}) collective-permute-start(bf16[64,4096]{1,0:T(8,128)(2,1)S(1)} %copy-done.1), channel_id=1, source_target_pairs={{0,2},{1,3},{2,0},{3,1},{4,6},{5,7},{6,4},{7,5},{8,10},{9,11},{10,... | collective-permute-start | bytes 1572872 | tf_op jit(solution)/shard_map/ppermute | solution.py:152
  20.6 35.7 %collective-permute-start.2 = (bf16[64,4096]{1,0:T(8,128)(2,1)S(1)}, bf16[64,4096]{1,0:T(8,128)(2,1)S(1)}, u32[]{:S(2)}, u32[]{:S(2)}) collective-permute-start(bf16[64,4096]{1,0:T(8,128)(2,1)S(1)} %copy-done.1), channel_id=1, source_target_pairs={{0,1},{1,0},{2,3},{3,2},{4,5},{5,4},{6,7},{7,6},{8,9},{9,8},{10,11... | collective-permute-start | bytes 1572872 | tf_op jit(solution)/shard_map/ppermute | solution.py:153
  55.3 1.9 %collective-permute-start.3 = (bf16[64,4096]{1,0:T(8,128)(2,1)S(1)}, bf16[64,4096]{1,0:T(8,128)(2,1)S(1)}, u32[]{:S(2)}, u32[]{:S(2)}) collective-permute-start(bf16[64,4096]{1,0:T(8,128)(2,1)S(1)} %collective-permute-done.1.x1), channel_id=1, source_target_pairs={{0,1},{1,0},{2,3},{3,2},{4,5},{5,4},{6,7},{7,6},{8,9},{9,8},{10,11... | collective-permute-start | bytes 1572872 | tf_op jit(solution)/shard_map/ppermute | solution.py:156

commit v2 on v0

v2 whole, which is shorter than its diff:
```python
import jax
import jax.numpy as jnp
from jax import lax
from jax.experimental import pallas as pl
from jax.experimental.pallas import tpu as pltpu
from jax.sharding import PartitionSpec as P


MESH = pl.DeviceIdType.MESH
CROSS = [(0, 2), (1, 3), (2, 0), (3, 1)]
SIBLING = [(0, 1), (1, 0), (2, 3), (3, 2)]
CHUNK = 512


def neighbours():
    me = lax.axis_index("tp")
    sib = me + 1 - 2 * lax.rem(me, 2)
    return me, lax.rem(me + 2, 4), sib, lax.rem(sib + 2, 4)


def dx_kernel(g_ref, w_ref, far_ref, near_ref, g_buf, w_buf, own, send, recv, g_sem, w_sem, send_sem, recv_sem):
    order = neighbours()
    sib = order[2]
    tokens, ffn = g_ref.shape[0] // 4, g_ref.shape[1]
    slots, chunk = w_buf.shape[0] // CHUNK, CHUNK
    chunks = w_ref.shape[0] // chunk
    halves = (pl.ds(0, ffn // 2), pl.ds(ffn // 2, ffn // 2))

    def fetch_g(k):
        return [
            pltpu.make_async_copy(
                g_ref.at[pl.ds(pl.multiple_of(idx * tokens, tokens), tokens), halves[k]],
                g_buf.at[pl.ds(j * tokens, tokens), halves[k]], g_sem.at[j, k])
            for j, idx in enumerate(order)]

    def fetch_half(c, k):
        return pltpu.make_async_copy(
            w_ref.at[pl.ds(c * chunk, chunk), halves[k]],
            w_buf.at[pl.ds(c % slots * chunk, chunk), halves[k]], w_sem.at[c % slots, k])

    def fetch(c):
        return pltpu.make_async_copy(
            w_ref.at[pl.ds(pl.multiple_of(c * chunk, chunk), chunk)],
            w_buf.at[pl.ds(pl.multiple_of(lax.rem(c, slots) * chunk, chunk), chunk)], w_sem.at[lax.rem(c, slots), 0])

    def to_sibling(c):
        return pltpu.make_async_remote_copy(
            src_ref=send.at[c], dst_ref=recv.at[c], send_sem=send_sem.at[c], recv_sem=recv_sem.at[c],
            device_id={"tp": sib}, device_id_type=MESH)

    def product(g, w):
        return lax.dot_general(g, w, (((1,), (1,)), ((), ())), preferred_element_type=jnp.float32)

    def keep(c, part):
        own[c] = part[: 2 * tokens]
        send[c] = part[2 * tokens:]

    def finish(c):
        to_sibling(c).wait_recv()
        cols = pl.ds(pl.multiple_of(c * chunk, chunk), chunk)
        near_ref[:, cols] = own[c, :tokens] + recv[c, :tokens]
        far_ref[:, cols] = own[c, tokens:] + recv[c, tokens:]

    for k in range(2):
        for copy in fetch_g(k):
            copy.start()
        fetch_half(0, k).start()
    for c in range(1, slots):
        fetch(c).start()

    barrier = pltpu.get_barrier_semaphore()
    pl.semaphore_signal(barrier, inc=1, device_id={"tp": sib}, device_id_type=MESH)
    pl.semaphore_wait(barrier, 1)

    def by_halves(c):
        for k in range(2):
            if c == 0:
                for copy in fetch_g(k):
                    copy.wait()
            fetch_half(c, k).wait()
            part = product(g_buf[:, halves[k]], w_buf[pl.ds(c % slots * chunk, chunk), halves[k]])
            if k:
                part = part + jnp.concatenate([own[c], send[c]], axis=0)
            keep(c, part)
        to_sibling(c).start()

    by_halves(0)
    fetch(slots).start()

    def pair(i, carry):
        c = 2 * i + 1
        fetch(c).wait()
        fetch(c + 1).wait()
        rows = pl.ds(pl.multiple_of(lax.rem(c, slots) * chunk, chunk), 2 * chunk)
        part = product(g_buf[...], w_buf[rows])
        keep(c, part[:, :chunk])
        keep(c + 1, part[:, chunk:])
        for d in (0, 1):
            @pl.when(c + d + slots < chunks - 1)
            def _():
                fetch(c + d + slots).start()

        @pl.when(c + 1 + slots == chunks - 1)
        def _():
            fetch_half(chunks - 1, 0).start()
            fetch_half(chunks - 1, 1).start()

        finish(c - 1)

        @pl.when(c >= 2)
        def _():
            finish(c - 2)

        to_sibling(c).start()
        to_sibling(c + 1).start()
        return carry

    lax.fori_loop(0, (chunks - 2) // 2, pair, 0)
    by_halves(chunks - 1)
    for c in range(chunks - 3, chunks):
        finish(c)
    for c in range(chunks):
        to_sibling(c).wait_send()


def dx_partial(g, w, slots=5):
    tokens, (hidden, ffn) = g.shape[0] // 4, w.shape
    chunks = hidden // CHUNK
    piece = jax.ShapeDtypeStruct((tokens, hidden), jnp.float32)
    sums = pltpu.VMEM((chunks, 2 * tokens, CHUNK), jnp.float32)
    return pl.pallas_call(
        dx_kernel,
        out_shape=(piece, piece, jax.ShapeDtypeStruct(g.shape, g.dtype)),
        in_specs=[pl.BlockSpec(memory_space=pl.ANY)] * 2,
        out_specs=[pl.BlockSpec(memory_space=pltpu.VMEM)] * 3,
        scratch_shapes=[
            pltpu.VMEM((slots * CHUNK, ffn), w.dtype),
            sums, sums, sums,
            pltpu.SemaphoreType.DMA((4, 2)),
            pltpu.SemaphoreType.DMA((slots, 2)),
            pltpu.SemaphoreType.DMA((chunks,)),
            pltpu.SemaphoreType.DMA((chunks,)),
        ],
        cost_estimate=pl.CostEstimate(
            flops=2 * g.shape[0] * hidden * ffn, bytes_accessed=2 * hidden * ffn, transcendentals=0),
        compiler_params=pltpu.CompilerParams(
            collective_id=0, has_side_effects=True, vmem_limit_bytes=49 * 1024 * 1024),
        name="dx_partial",
    )(g, w)


def dw_kernel(x0, x1, x2, x3, g_ref, out_ref, x_buf, out_buf, out_sem):
    tokens, hidden = x0.shape
    slots, rows = out_buf.shape[0], out_buf.shape[1]
    steps = hidden // rows
    for j, x in enumerate((x0, x1, x2, x3)):
        x_buf[j * tokens:(j + 1) * tokens] = x[...]

    def put(i):
        return pltpu.make_async_copy(
            out_buf.at[lax.rem(i, slots)], out_ref.at[pl.ds(pl.multiple_of(i * rows, rows), rows)],
            out_sem.at[lax.rem(i, slots)])

    def step(i, carry):
        @pl.when(i >= slots)
        def _():
            put(i - slots).wait()

        out_buf[lax.rem(i, slots)] = lax.dot_general(
            x_buf[:, pl.ds(pl.multiple_of(i * rows, rows), rows)], g_ref[...],
            (((0,), (0,)), ((), ())), preferred_element_type=jnp.float32)
        put(i).start()
        return carry

    lax.fori_loop(0, steps, step, 0)
    for i in range(steps - slots, steps):
        put(i).wait()


def dw(blocks, g, rows=128, slots=8):
    tokens, hidden = blocks[0].shape
    ffn = g.shape[1]
    return pl.pallas_call(
        dw_kernel,
        out_shape=jax.ShapeDtypeStruct((hidden, ffn), jnp.float32),
        in_specs=[pl.BlockSpec(memory_space=pltpu.VMEM)] * 5,
        out_specs=pl.BlockSpec(memory_space=pltpu.HBM),
        scratch_shapes=[
            pltpu.VMEM((4 * tokens, hidden), g.dtype),
            pltpu.VMEM((slots, rows, ffn), jnp.float32),
            pltpu.SemaphoreType.DMA((slots,)),
        ],
        cost_estimate=pl.CostEstimate(
            flops=8 * tokens * hidden * ffn, bytes_accessed=4 * hidden * ffn, transcendentals=0),
        compiler_params=pltpu.CompilerParams(vmem_limit_bytes=40 * 1024 * 1024),
        name="dw",
    )(*blocks, g)


def solution(mesh):
    def per_device(x, w, g):
        x_cross = lax.ppermute(x, "tp", CROSS)
        x_sib = lax.ppermute(x, "tp", SIBLING)
        far, near, g_here = dx_partial(g, w)
        arrived = lax.ppermute(far, "tp", CROSS)
        x_last = lax.ppermute(x_cross, "tp", SIBLING)
        grad_w = dw((x, x_cross, x_sib, x_last), g_here)
        return (near + arrived).astype(jnp.bfloat16), grad_w

    return jax.shard_map(
        per_device,
        mesh=mesh,
        in_specs=(P(("dp", "tp"), None), P(None, "tp"), P("dp", "tp")),
        out_specs=(P(("dp", "tp"), None), P("dp", "tp")),
        check_vma=False,
    )
```

time: 85.6 us -> 79.8 us (0.932)
  matrix products: 44.3 us -> 0 us
  Pallas kernels: 0 us -> 39.5 us
  between operations: 14 us -> 0.65 us
  waiting for transfers between devices: 24 us -> 35.8 us
  starting transfers between devices: 0.08 us -> 2.8 us
  other arithmetic: 2.07 us -> 0.89 us
    dot_general x2 -> x0, matrix products: 44.3 us -> none  [the longest x1 27.6 us: per_device(): lax.dot_general(x_full, grad_blk, (((0,), (0,)), ((), ())), preferred_ele...]
    pallas_call x0 -> x2, Pallas kernels: none -> 39.5 us  [the longest x1 21.7 us: dw(): pl.pallas_call(dw_kernel, out_shape=jax.ShapeDtypeStruct((hidden, ffn), j...]
    ppermute x0 -> x4, waiting for transfers between devices: none -> 35.8 us  [the longest x1 34.8 us: per_device(): x_cross = lax.ppermute(x, 'tp', CROSS)]
    reduce_scatter x1 -> x0, waiting for transfers between devices: 15.8 us -> none  [per_device(): lax.psum_scatter(part_dx, 'tp', scatter_dimension=0, tiled=True)]
    all_gather x1 -> x0, waiting for transfers between devices: 7.46 us -> none  [per_device(): x_full = lax.all_gather(x_blk, 'tp', axis=0, tiled=True)]
    ppermute x0 -> x4, starting transfers between devices: none -> 2.8 us  [the longest x1 2.61 us: per_device(): arrived = lax.ppermute(far, 'tp', CROSS)]
    convert_element_type x1, other arithmetic: 2.07 us -> 0.89 us  [per_device(): return ((near + arrived).astype(jnp.bfloat16), grad_w)]
  transfers between devices with their start and end apart: 2 -> 4, of which waited for: 2 -> 2; matrix products, arithmetic and copies ran while one was open for 52% -> 1% of each run, Pallas kernels for 0% -> 0%
where the time goes in v2:
time: 79.8 us; the launch traced here: 79.7 us
  Pallas kernels  39.5 us (49%)
  waiting for transfers between devices  35.8 us (45%)
  starting transfers between devices  2.8 us (4%)
  other arithmetic  0.89 us (1%)
    ppermute x1, waiting for transfers between devices, per_device(): x_cross = lax.ppermute(x, 'tp', CROSS)  34.8 us
    pallas_call x1, Pallas kernels, dw(): pl.pallas_call(dw_kernel, out_shape=jax.ShapeDtypeStruct((hidden, ffn), j...  21.7 us
    pallas_call x1, Pallas kernels, dx_partial(): pl.pallas_call(dx_kernel, out_shape=(piece, piece, jax.ShapeDtypeStruct(g...  17.9 us
    ppermute x1, starting transfers between devices, per_device(): arrived = lax.ppermute(far, 'tp', CROSS)  2.61 us
  transfers between devices with their start and end apart: 4, of which 2 were waited for; matrix products, arithmetic and copies ran while one was open for 1% of the time, Pallas kernels for 0%

profile of v2, /device:TPU:0, one launch (start us, length us, event | category | flops | bytes accessed | tf_op | source)
XLA Modules:
  0.0 79.7 jit_solution(18114046094427766757)
XLA Ops:
  0.6 0.0 copy-start
  0.6 17.9 %dx_partial.1 = (f32[64,4096]{1,0:T(8,128)S(1)}, f32[64,4096]{1,0:T(8,128)S(1)}, bf16[256,4096]{1,0:T(8,128)(2,1)S(1)}) custom-call(bf16[256,4096]{1,0:T(8,128)(2,1)} %g_ref.1, bf16[4096,4096]{1,0:T(8,128)(2,1)} %w_ref.1), custom_call_target="tpu_custom_call" | custom-call | flops 8589934592 | bytes 33554432 | tf_op jit(solution)/shard_map/dx_partial/pallas_call | solution.py:131
  18.5 2.6 %collective-permute-start = (f32[64,4096]{1,0:T(8,128)S(1)}, f32[64,4096]{1,0:T(8,128)S(1)}, u32[]{:S(2)}, u32[]{:S(2)}) collective-permute-start(f32[64,4096]{1,0:T(8,128)S(1)} %get-tuple-element.6), channel_id=1, source_target_pairs={{0,2},{1,3},{2,0},{3,1},{4,6},{5,7},{6,4},{7,5},{8,10},{9,11},{10,... | collective-permute-start | bytes 3145736 | tf_op jit(solution)/shard_map/ppermute | solution.py:205
  21.1 0.0 copy-done
  21.1 0.1 collective-permute-start.1
  21.2 0.1 collective-permute-start.2
  21.3 34.8 %collective-permute-done.1.x1 = bf16[64,4096]{1,0:T(8,128)(2,1)S(1)} collective-permute-done((bf16[64,4096]{1,0:T(8,128)(2,1)S(1)}, bf16[64,4096]{1,0:T(8,128)(2,1)S(1)}, u32[]{:S(2)}, u32[]{:S(2)}) %collective-permute-start.1) | collective-permute-done | bytes 524320 | tf_op jit(solution)/shard_map/ppermute | solution.py:202
  56.1 0.0 collective-permute-start.3
  56.1 0.0 collective-permute-done
  56.1 0.9 %add_convert_fusion = bf16[64,4096]{1,0:T(8,128)(2,1)} fusion(f32[64,4096]{1,0:T(8,128)S(1)} %get-tuple-element.5, f32[64,4096]{1,0:T(8,128)S(1)} %collective-permute-done), kind=kLoop, calls=%fused_computation | loop fusion | flops 524288 | bytes 2621440 | tf_op jit(solution)/shard_map/convert_element_type | solution.py:208
  57.0 0.0 collective-permute-done.2.x2
  57.0 1.0 %collective-permute-done.3.x3 = bf16[64,4096]{1,0:T(8,128)(2,1)S(1)} collective-permute-done((bf16[64,4096]{1,0:T(8,128)(2,1)S(1)}, bf16[64,4096]{1,0:T(8,128)(2,1)S(1)}, u32[]{:S(2)}, u32[]{:S(2)}) %collective-permute-start.3) | collective-permute-done | bytes 524320 | tf_op jit(solution)/shard_map/ppermute | solution.py:206
  58.0 21.7 %dw.1 = f32[4096,4096]{1,0:T(8,128)} custom-call(bf16[64,4096]{1,0:T(8,128)(2,1)S(1)} %copy-done, bf16[64,4096]{1,0:T(8,128)(2,1)S(1)} %collective-permute-done.1.x1, bf16[64,4096]{1,0:T(8,128)(2,1)S(1)} %collective-permute-done.2.x2, bf16[64,4096]{1,0:T(8,128)(2,1)S(1)} %collective-permute-done.3.x3, bf16[256,4096]{1,0:T(8,128)(2,1)S(1)} %get-tuple-element.7.g_ref), custom_call_target="tpu_custom_call" | custom-call | flops 8589934592 | bytes 67108864 | tf_op jit(solution)/shard_map/dw/pallas_call | solution.py:183
Async XLA Ops:
  0.6 20.5 %copy-start = (bf16[64,4096]{1,0:T(8,128)(2,1)S(1)}, bf16[64,4096]{1,0:T(8,128)(2,1)}, u32[]{:S(2)}) copy-start(bf16[64,4096]{1,0:T(8,128)(2,1)} %x0.1) | copy-start | bytes 1572868
  18.5 37.6 %collective-permute-start = (f32[64,4096]{1,0:T(8,128)S(1)}, f32[64,4096]{1,0:T(8,128)S(1)}, u32[]{:S(2)}, u32[]{:S(2)}) collective-permute-start(f32[64,4096]{1,0:T(8,128)S(1)} %get-tuple-element.6), channel_id=1, source_target_pairs={{0,2},{1,3},{2,0},{3,1},{4,6},{5,7},{6,4},{7,5},{8,10},{9,11},{10,... | collective-permute-start | bytes 3145736 | tf_op jit(solution)/shard_map/ppermute | solution.py:205
  21.1 35.0 %collective-permute-start.1 = (bf16[64,4096]{1,0:T(8,128)(2,1)S(1)}, bf16[64,4096]{1,0:T(8,128)(2,1)S(1)}, u32[]{:S(2)}, u32[]{:S(2)}) collective-permute-start(bf16[64,4096]{1,0:T(8,128)(2,1)S(1)} %copy-done), channel_id=1, source_target_pairs={{0,2},{1,3},{2,0},{3,1},{4,6},{5,7},{6,4},{7,5},{8,10},{9,11},{10,... | collective-permute-start | bytes 1572872 | tf_op jit(solution)/shard_map/ppermute | solution.py:202
  21.2 35.8 %collective-permute-start.2 = (bf16[64,4096]{1,0:T(8,128)(2,1)S(1)}, bf16[64,4096]{1,0:T(8,128)(2,1)S(1)}, u32[]{:S(2)}, u32[]{:S(2)}) collective-permute-start(bf16[64,4096]{1,0:T(8,128)(2,1)S(1)} %copy-done), channel_id=1, source_target_pairs={{0,1},{1,0},{2,3},{3,2},{4,5},{5,4},{6,7},{7,6},{8,9},{9,8},{10,11... | collective-permute-start | bytes 1572872 | tf_op jit(solution)/shard_map/ppermute | solution.py:203
  56.1 1.9 %collective-permute-start.3 = (bf16[64,4096]{1,0:T(8,128)(2,1)S(1)}, bf16[64,4096]{1,0:T(8,128)(2,1)S(1)}, u32[]{:S(2)}, u32[]{:S(2)}) collective-permute-start(bf16[64,4096]{1,0:T(8,128)(2,1)S(1)} %collective-permute-done.1.x1), channel_id=1, source_target_pairs={{0,1},{1,0},{2,3},{3,2},{4,5},{5,4},{6,7},{7,6},{8,9},{9,8},{10,11... | collective-permute-start | bytes 1572872 | tf_op jit(solution)/shard_map/ppermute | solution.py:206

commit v3 on v0

v3 whole, which is shorter than its diff:
```python
import jax
import jax.numpy as jnp
from jax import lax
from jax.experimental import pallas as pl
from jax.experimental.pallas import tpu as pltpu
from jax.sharding import PartitionSpec as P


MESH = pl.DeviceIdType.MESH
CROSS = [(0, 2), (1, 3), (2, 0), (3, 1)]
CHUNK = 512
SLOTS = 5
PIECES = 4
EARLY = 1


def neighbours():
    me = lax.axis_index("tp")
    sib = me + 1 - 2 * lax.rem(me, 2)
    return me, lax.rem(me + 2, 4), sib, lax.rem(sib + 2, 4)


def front_kernel(x_ref, g_ref, w_ref, near_ref, far_ref, early_ref, x_all, g_all,
                 w_buf, own, send, recv, early_src,
                 x_sem, g_sem, w_sem, sum_send, sum_recv, sib_send, sib_recv,
                 cross_send, cross_recv, last_send, last_recv, early_send, early_recv):
    order = neighbours()
    _, cross, sib, _ = order
    tokens = x_ref.shape[0]
    chunks = w_ref.shape[0] // CHUNK
    piece = x_ref.shape[1] // PIECES

    def remote(src, dst, send_sem, recv_sem, to):
        return pltpu.make_async_remote_copy(
            src_ref=src, dst_ref=dst, send_sem=send_sem, recv_sem=recv_sem,
            device_id={"tp": to}, device_id_type=MESH)

    def block(j):
        return pl.ds(j * tokens, tokens)

    def chunk_of(c):
        return pl.ds(pl.multiple_of(c * CHUNK, CHUNK), CHUNK)

    fetch_x = pltpu.make_async_copy(x_ref, x_all.at[block(0)], x_sem)
    fetch_g = [
        pltpu.make_async_copy(
            g_ref.at[pl.ds(pl.multiple_of(idx * tokens, tokens), tokens)], g_all.at[block(j)], g_sem.at[j])
        for j, idx in enumerate(order)]

    def fetch_w(c):
        slot = lax.rem(c, SLOTS)
        return pltpu.make_async_copy(w_ref.at[chunk_of(c)], w_buf.at[slot], w_sem.at[slot])

    def cross_piece(p):
        cols = pl.ds(p * piece, piece)
        return remote(x_ref.at[:, cols], x_all.at[block(1), cols], cross_send.at[p], cross_recv.at[p], cross)

    def last_piece(p):
        cols = pl.ds(p * piece, piece)
        return remote(x_all.at[block(1), cols], x_all.at[block(3), cols], last_send.at[p], last_recv.at[p], sib)

    def to_sibling(c):
        return remote(send.at[c], recv.at[c], sum_send.at[c], sum_recv.at[c], sib)

    def early(c):
        return remote(early_src.at[c], early_ref.at[c], early_send.at[c], early_recv.at[c], cross)

    x_to_sibling = remote(x_ref, x_all.at[block(2)], sib_send, sib_recv, sib)

    for copy in fetch_g:
        copy.start()
    for c in range(SLOTS):
        fetch_w(c).start()

    barrier = pltpu.get_barrier_semaphore()
    for to in (sib, cross):
        pl.semaphore_signal(barrier, inc=1, device_id={"tp": to}, device_id_type=MESH)
    pl.semaphore_wait(barrier, 2)
    for p in range(PIECES):
        cross_piece(p).start()
    x_to_sibling.start()
    fetch_x.start()
    for copy in fetch_g:
        copy.wait()

    def forward(p):
        cross_piece(p).wait_recv()
        last_piece(p).start()

    def finish(c):
        to_sibling(c).wait_recv()
        near_ref[:, chunk_of(c)] = own[c, :tokens] + recv[c, :tokens]
        total = own[c, tokens:] + recv[c, tokens:]

        @pl.when(c < EARLY)
        def _():
            early_src[0] = total

        @pl.when(c >= EARLY)
        def _():
            far_ref[:, chunk_of(c - EARLY)] = total

    def step(c, carry):
        fetch_w(c).wait()
        part = lax.dot_general(g_all[...], w_buf[lax.rem(c, SLOTS)], (((1,), (1,)), ((), ())),
                               preferred_element_type=jnp.float32)
        own[c] = part[:2 * tokens]
        send[c] = part[2 * tokens:]

        @pl.when(c + SLOTS < chunks)
        def _():
            fetch_w(c + SLOTS).start()

        @pl.when(c >= 1)
        def _():
            finish(c - 1)

        to_sibling(c).start()
        for p in range(PIECES - 1):
            @pl.when(c == 2 * p + 2)
            def _():
                forward(p)

        @pl.when(c == 2)
        def _():
            early(0).start()

        return carry

    lax.fori_loop(0, chunks, step, 0)
    finish(chunks - 1)
    forward(PIECES - 1)
    x_to_sibling.wait()
    fetch_x.wait()
    for c in range(chunks):
        to_sibling(c).wait_send()
    for c in range(EARLY):
        early(c).wait()
    for p in range(PIECES):
        cross_piece(p).wait_send()
        last_piece(p).wait()


def front(x, g, w):
    tokens, (hidden, ffn) = x.shape[0], w.shape
    chunks = hidden // CHUNK
    dma = pltpu.SemaphoreType.DMA
    sums = pltpu.VMEM((chunks, 2 * tokens, CHUNK), jnp.float32)
    return pl.pallas_call(
        front_kernel,
        out_shape=(
            jax.ShapeDtypeStruct((tokens, hidden), jnp.float32),
            jax.ShapeDtypeStruct((tokens, hidden - EARLY * CHUNK), jnp.float32),
            jax.ShapeDtypeStruct((EARLY, tokens, CHUNK), jnp.float32),
            jax.ShapeDtypeStruct((4 * tokens, hidden), x.dtype),
            jax.ShapeDtypeStruct(g.shape, g.dtype),
        ),
        in_specs=[pl.BlockSpec(memory_space=pl.ANY)] * 3,
        out_specs=[pl.BlockSpec(memory_space=pltpu.VMEM)] * 5,
        scratch_shapes=[
            pltpu.VMEM((SLOTS, CHUNK, ffn), w.dtype),
            sums, sums, sums,
            pltpu.VMEM((EARLY, tokens, CHUNK), jnp.float32),
            dma, dma((4,)), dma((SLOTS,)), dma((chunks,)), dma((chunks,)), dma, dma,
            dma((PIECES,)), dma((PIECES,)), dma((PIECES,)), dma((PIECES,)), dma((EARLY,)), dma((EARLY,)),
        ],
        cost_estimate=pl.CostEstimate(
            flops=2 * g.shape[0] * hidden * ffn, bytes_accessed=2 * hidden * ffn, transcendentals=0),
        compiler_params=pltpu.CompilerParams(
            collective_id=0, has_side_effects=True, vmem_limit_bytes=46 * 1024 * 1024),
        name="front",
    )(x, g, w)


def dw_kernel(x_ref, g_ref, out_ref, out_buf, out_sem):
    slots, rows = out_buf.shape[0], out_buf.shape[1]
    steps = x_ref.shape[1] // rows

    def put(i):
        return pltpu.make_async_copy(
            out_buf.at[lax.rem(i, slots)], out_ref.at[pl.ds(pl.multiple_of(i * rows, rows), rows)],
            out_sem.at[lax.rem(i, slots)])

    def step(i, carry):
        @pl.when(i >= slots)
        def _():
            put(i - slots).wait()

        out_buf[lax.rem(i, slots)] = lax.dot_general(
            x_ref[:, pl.ds(pl.multiple_of(i * rows, rows), rows)], g_ref[...],
            (((0,), (0,)), ((), ())), preferred_element_type=jnp.float32)
        put(i).start()
        return carry

    lax.fori_loop(0, steps, step, 0)
    for i in range(steps - slots, steps):
        put(i).wait()


def dw(x, g, rows=128, slots=8):
    tokens, hidden = x.shape
    ffn = g.shape[1]
    return pl.pallas_call(
        dw_kernel,
        out_shape=jax.ShapeDtypeStruct((hidden, ffn), jnp.float32),
        in_specs=[pl.BlockSpec(memory_space=pltpu.VMEM)] * 2,
        out_specs=pl.BlockSpec(memory_space=pl.ANY),
        scratch_shapes=[
            pltpu.VMEM((slots, rows, ffn), jnp.float32),
            pltpu.SemaphoreType.DMA((slots,)),
        ],
        cost_estimate=pl.CostEstimate(
            flops=2 * tokens * hidden * ffn, bytes_accessed=4 * hidden * ffn, transcendentals=0),
        compiler_params=pltpu.CompilerParams(vmem_limit_bytes=40 * 1024 * 1024),
        name="dw",
    )(x, g)


def solution(mesh):
    def per_device(x, w, g):
        near, far, early, x_all, g_all = front(x, g, w)
        arrived = lax.ppermute(far, "tp", CROSS)
        grad_w = dw(x_all, g_all)
        arrived = jnp.concatenate([early[c] for c in range(EARLY)] + [arrived], axis=1)
        return (near + arrived).astype(jnp.bfloat16), grad_w

    return jax.shard_map(
        per_device,
        mesh=mesh,
        in_specs=(P(("dp", "tp"), None), P(None, "tp"), P("dp", "tp")),
        out_specs=(P(("dp", "tp"), None), P("dp", "tp")),
        check_vma=False,
    )
```

time: 85.6 us -> 47.3 us (0.55)
  matrix products: 44.3 us -> 0 us
  Pallas kernels: 0 us -> 41.8 us
  waiting for transfers between devices: 24 us -> 0.01 us
  between operations: 14 us -> 0.66 us
  starting transfers between devices: 0.08 us -> 2.79 us
  other arithmetic: 2.07 us -> 0.89 us
    dot_general x2 -> x0, matrix products: 44.3 us -> none  [the longest x1 27.6 us: per_device(): lax.dot_general(x_full, grad_blk, (((0,), (0,)), ((), ())), preferred_ele...]
    pallas_call x0 -> x2, Pallas kernels: none -> 41.8 us  [the longest x1 21.5 us: dw(): pl.pallas_call(dw_kernel, out_shape=jax.ShapeDtypeStruct((hidden, ffn), j...]
    reduce_scatter x1 -> x0, waiting for transfers between devices: 15.8 us -> none  [per_device(): lax.psum_scatter(part_dx, 'tp', scatter_dimension=0, tiled=True)]
    all_gather x1 -> x0, waiting for transfers between devices: 7.46 us -> none  [per_device(): x_full = lax.all_gather(x_blk, 'tp', axis=0, tiled=True)]
    ppermute x0 -> x1, starting transfers between devices: none -> 2.79 us  [per_device(): arrived = lax.ppermute(far, 'tp', CROSS)]
    convert_element_type x1, other arithmetic: 2.07 us -> 0.89 us  [per_device(): return ((near + arrived).astype(jnp.bfloat16), grad_w)]
  transfers between devices with their start and end apart: 2 -> 1, of which waited for: 2 -> 0; matrix products, arithmetic and copies ran while one was open for 52% -> 0% of each run, Pallas kernels for 0% -> 46%
where the time goes in v3:
time: 47.3 us; the launch traced here: 47.2 us
  Pallas kernels  41.8 us (88%)
  starting transfers between devices  2.79 us (6%)
  local copies, waits for them, and re-layouts  1.03 us (2%)
  other arithmetic  0.89 us (2%)
  between operations  0.66 us (1%)
    pallas_call x1, Pallas kernels, dw(): pl.pallas_call(dw_kernel, out_shape=jax.ShapeDtypeStruct((hidden, ffn), j...  21.5 us
    pallas_call x1, Pallas kernels, front(): pl.pallas_call(front_kernel, out_shape=(jax.ShapeDtypeStruct((tokens, hid...  20.3 us
    ppermute x1, starting transfers between devices, per_device(): arrived = lax.ppermute(far, 'tp', CROSS)  2.79 us
    unnamed x2, local copies, waits for them, and re-layouts  1.03 us
  transfers between devices with their start and end apart: 1, of which 0 were waited for; matrix products, arithmetic and copies ran while one was open for 0% of the time, Pallas kernels for 46%

profile of v3, /device:TPU:0, one launch (start us, length us, event | category | flops | bytes accessed | tf_op | source)
XLA Modules:
  0.0 47.2 jit_solution(5826809709379285355)
XLA Ops:
  0.6 0.0 copy-start
  0.6 1.0 %copy-done = bf16[64,4096]{1,0:T(8,128)(2,1)S(1)} copy-done((bf16[64,4096]{1,0:T(8,128)(2,1)S(1)}, bf16[64,4096]{1,0:T(8,128)(2,1)}, u32[]{:S(2)}) %copy-start) | copy-done | bytes 524312
  1.7 20.3 %front.1 = (f32[64,4096]{1,0:T(8,128)S(1)}, f32[64,3584]{1,0:T(8,128)S(1)}, f32[1,64,512]{2,1,0:T(8,128)S(1)}, bf16[256,4096]{1,0:T(8,128)(2,1)S(1)}, bf16[256,4096]{1,0:T(8,128)(2,1)S(1)}) custom-call(bf16[64,4096]{1,0:T(8,128)(2,1)S(1)} %copy-done, bf16[256,4096]{1,0:T(8,128)(2,1)} %g_ref.1, bf16[4096,4096]{1,0:T(8,128)(2,1)} %w_ref.1), custom_call_target="tpu_custom_call" | custom-call | flops 8589934592 | bytes 33554432 | tf_op jit(solution)/shard_map/front/pallas_call | solution.py:149
  21.9 2.8 %collective-permute-start = (f32[64,3584]{1,0:T(8,128)S(1)}, f32[64,3584]{1,0:T(8,128)S(1)}, u32[]{:S(2)}, u32[]{:S(2)}) collective-permute-start(f32[64,3584]{1,0:T(8,128)S(1)} %get-tuple-element.9), channel_id=1, source_target_pairs={{0,2},{1,3},{2,0},{3,1},{4,6},{5,7},{6,4},{7,5},{8,10},{9,11},{10,... | collective-permute-start | bytes 2752520 | tf_op jit(solution)/shard_map/ppermute | solution.py:222
  24.7 21.5 %dw.1 = f32[4096,4096]{1,0:T(8,128)} custom-call(bf16[256,4096]{1,0:T(8,128)(2,1)S(1)} %get-tuple-element.10.x_ref, bf16[256,4096]{1,0:T(8,128)(2,1)S(1)} %get-tuple-element.11.g_ref), custom_call_target="tpu_custom_call" | custom-call | flops 8589934592 | bytes 67108864 | tf_op jit(solution)/shard_map/dw/pallas_call | solution.py:203
  46.3 0.0 collective-permute-done
  46.3 0.9 %fusion = bf16[64,4096]{1,0:T(8,128)(2,1)} fusion(f32[64,4096]{1,0:T(8,128)S(1)} %get-tuple-element.7, f32[64,3584]{1,0:T(8,128)S(1)} %collective-permute-done, f32[64,512]{1,0:T(8,128)S(1)} %bitcast.1), kind=kLoop, calls=%fused_computation.1 | loop fusion | flops 786432 | bytes 2621440 | tf_op jit(solution)/shard_map/convert_element_type | solution.py:225
Async XLA Ops:
  0.6 1.0 %copy-start = (bf16[64,4096]{1,0:T(8,128)(2,1)S(1)}, bf16[64,4096]{1,0:T(8,128)(2,1)}, u32[]{:S(2)}) copy-start(bf16[64,4096]{1,0:T(8,128)(2,1)} %x_ref.1) | copy-start | bytes 1572868
  21.9 24.3 %collective-permute-start = (f32[64,3584]{1,0:T(8,128)S(1)}, f32[64,3584]{1,0:T(8,128)S(1)}, u32[]{:S(2)}, u32[]{:S(2)}) collective-permute-start(f32[64,3584]{1,0:T(8,128)S(1)} %get-tuple-element.9), channel_id=1, source_target_pairs={{0,2},{1,3},{2,0},{3,1},{4,6},{5,7},{6,4},{7,5},{8,10},{9,11},{10,... | collective-permute-start | bytes 2752520 | tf_op jit(solution)/shard_map/ppermute | solution.py:222

commit v4 on v3

--- a/solution.py
+++ b/solution.py
@@ -9,7 +9,7 @@
 MESH = pl.DeviceIdType.MESH
 CROSS = [(0, 2), (1, 3), (2, 0), (3, 1)]
 CHUNK = 512
-SLOTS = 5
+SLOTS = 3
 PIECES = 4
 EARLY = 1
 
@@ -67,11 +67,6 @@
 
     x_to_sibling = remote(x_ref, x_all.at[block(2)], sib_send, sib_recv, sib)
 
-    for copy in fetch_g:
-        copy.start()
-    for c in range(SLOTS):
-        fetch_w(c).start()
-
     barrier = pltpu.get_barrier_semaphore()
     for to in (sib, cross):
         pl.semaphore_signal(barrier, inc=1, device_id={"tp": to}, device_id_type=MESH)
@@ -79,6 +74,10 @@
     for p in range(PIECES):
         cross_piece(p).start()
     x_to_sibling.start()
+    for copy in fetch_g:
+        copy.start()
+    for c in range(2):
+        fetch_w(c).start()
     fetch_x.start()
     for copy in fetch_g:
         copy.wait()
@@ -102,14 +101,15 @@
 
     def step(c, carry):
         fetch_w(c).wait()
+
+        @pl.when(c + 2 < chunks)
+        def _():
+            fetch_w(c + 2).start()
+
         part = lax.dot_general(g_all[...], w_buf[lax.rem(c, SLOTS)], (((1,), (1,)), ((), ())),
                                preferred_element_type=jnp.float32)
         own[c] = part[:2 * tokens]
         send[c] = part[2 * tokens:]
-
-        @pl.when(c + SLOTS < chunks)
-        def _():
-            fetch_w(c + SLOTS).start()
 
         @pl.when(c >= 1)
         def _():

time: 47.3 us -> 44.8 us (0.947)
  starting transfers between devices: 2.79 us -> 0.58 us
  Pallas kernels: 41.8 us -> 41.1 us
    ppermute x1, starting transfers between devices: 2.79 us -> 0.58 us  [per_device(): arrived = lax.ppermute(far, 'tp', CROSS)]
    pallas_call x1, Pallas kernels: 20.3 us -> 19.5 us  [front(): pl.pallas_call(front_kernel, out_shape=(jax.ShapeDtypeStruct((tokens, hid...]
  transfers between devices with their start and end apart: 1 -> 1, of which waited for: 0 -> 1; matrix products, arithmetic and copies ran while one was open for 0% -> 0% of each run, Pallas kernels for 46% -> 48%
where the time goes in v4:
time: 44.8 us; the launch traced here: 44.6 us
  Pallas kernels  41.1 us (92%)
  local copies, waits for them, and re-layouts  1.03 us (2%)
  other arithmetic  0.89 us (2%)
  between operations  0.66 us (1%)
  starting transfers between devices  0.58 us (1%)
    pallas_call x1, Pallas kernels, dw(): pl.pallas_call(dw_kernel, out_shape=jax.ShapeDtypeStruct((hidden, ffn), j...  21.5 us
    pallas_call x1, Pallas kernels, front(): pl.pallas_call(front_kernel, out_shape=(jax.ShapeDtypeStruct((tokens, hid...  19.5 us
    unnamed x2, local copies, waits for them, and re-layouts  1.03 us
  transfers between devices with their start and end apart: 1, of which 1 were waited for; matrix products, arithmetic and copies ran while one was open for 0% of the time, Pallas kernels for 48%

profile of v4, /device:TPU:0, one launch (start us, length us, event | category | flops | bytes accessed | tf_op | source)
XLA Modules:
  0.0 44.6 jit_solution(1062104060788555151)
XLA Ops:
  0.6 0.0 copy-start
  0.6 1.0 %copy-done = bf16[64,4096]{1,0:T(8,128)(2,1)S(1)} copy-done((bf16[64,4096]{1,0:T(8,128)(2,1)S(1)}, bf16[64,4096]{1,0:T(8,128)(2,1)}, u32[]{:S(2)}) %copy-start) | copy-done | bytes 524312
  1.7 19.5 %front.1 = (f32[64,4096]{1,0:T(8,128)S(1)}, f32[64,3584]{1,0:T(8,128)S(1)}, f32[1,64,512]{2,1,0:T(8,128)S(1)}, bf16[256,4096]{1,0:T(8,128)(2,1)S(1)}, bf16[256,4096]{1,0:T(8,128)(2,1)S(1)}) custom-call(bf16[64,4096]{1,0:T(8,128)(2,1)S(1)} %copy-done, bf16[256,4096]{1,0:T(8,128)(2,1)} %g_ref.1, bf16[4096,4096]{1,0:T(8,128)(2,1)} %w_ref.1), custom_call_target="tpu_custom_call" | custom-call | flops 8589934592 | bytes 33554432 | tf_op jit(solution)/shard_map/front/pallas_call | solution.py:149
  21.2 0.6 %collective-permute-start = (f32[64,3584]{1,0:T(8,128)S(1)}, f32[64,3584]{1,0:T(8,128)S(1)}, u32[]{:S(2)}, u32[]{:S(2)}) collective-permute-start(f32[64,3584]{1,0:T(8,128)S(1)} %get-tuple-element.9), channel_id=1, source_target_pairs={{0,2},{1,3},{2,0},{3,1},{4,6},{5,7},{6,4},{7,5},{8,10},{9,11},{10,... | collective-permute-start | bytes 2752520 | tf_op jit(solution)/shard_map/ppermute | solution.py:222
  21.8 21.5 %dw.1 = f32[4096,4096]{1,0:T(8,128)} custom-call(bf16[256,4096]{1,0:T(8,128)(2,1)S(1)} %get-tuple-element.10.x_ref, bf16[256,4096]{1,0:T(8,128)(2,1)S(1)} %get-tuple-element.11.g_ref), custom_call_target="tpu_custom_call" | custom-call | flops 8589934592 | bytes 67108864 | tf_op jit(solution)/shard_map/dw/pallas_call | solution.py:203
  43.3 0.4 collective-permute-done
  43.7 0.9 %fusion = bf16[64,4096]{1,0:T(8,128)(2,1)} fusion(f32[64,4096]{1,0:T(8,128)S(1)} %get-tuple-element.7, f32[64,3584]{1,0:T(8,128)S(1)} %collective-permute-done, f32[64,512]{1,0:T(8,128)S(1)} %bitcast.1), kind=kLoop, calls=%fused_computation.1 | loop fusion | flops 786432 | bytes 2621440 | tf_op jit(solution)/shard_map/convert_element_type | solution.py:225
Async XLA Ops:
  0.6 1.0 %copy-start = (bf16[64,4096]{1,0:T(8,128)(2,1)S(1)}, bf16[64,4096]{1,0:T(8,128)(2,1)}, u32[]{:S(2)}) copy-start(bf16[64,4096]{1,0:T(8,128)(2,1)} %x_ref.1) | copy-start | bytes 1572868
  21.2 22.5 %collective-permute-start = (f32[64,3584]{1,0:T(8,128)S(1)}, f32[64,3584]{1,0:T(8,128)S(1)}, u32[]{:S(2)}, u32[]{:S(2)}) collective-permute-start(f32[64,3584]{1,0:T(8,128)S(1)} %get-tuple-element.9), channel_id=1, source_target_pairs={{0,2},{1,3},{2,0},{3,1},{4,6},{5,7},{6,4},{7,5},{8,10},{9,11},{10,... | collective-permute-start | bytes 2752520 | tf_op jit(solution)/shard_map/ppermute | solution.py:222

commit v5 on v4

--- a/solution.py
+++ b/solution.py
@@ -11,7 +11,7 @@
 CHUNK = 512
 SLOTS = 3
 PIECES = 4
-EARLY = 1
+EARLY = 256
 
 
 def neighbours():
@@ -62,10 +62,19 @@
     def to_sibling(c):
         return remote(send.at[c], recv.at[c], sum_send.at[c], sum_recv.at[c], sib)
 
-    def early(c):
-        return remote(early_src.at[c], early_ref.at[c], early_send.at[c], early_recv.at[c], cross)
-
+    early = remote(early_src, early_ref, early_send, early_recv, cross)
     x_to_sibling = remote(x_ref, x_all.at[block(2)], sib_send, sib_recv, sib)
+
+    def first_reads():
+        for copy in fetch_g:
+            copy.start()
+        fetch_w(0).start()
+
+    upper = order[0] >= 2
+
+    @pl.when(jnp.logical_not(upper))
+    def _():
+        first_reads()
 
     barrier = pltpu.get_barrier_semaphore()
     for to in (sib, cross):
@@ -74,10 +83,12 @@
     for p in range(PIECES):
         cross_piece(p).start()
     x_to_sibling.start()
-    for copy in fetch_g:
-        copy.start()
-    for c in range(2):
-        fetch_w(c).start()
+
+    @pl.when(upper)
+    def _():
+        first_reads()
+
+    fetch_w(1).start()
     fetch_x.start()
     for copy in fetch_g:
         copy.wait()
@@ -91,13 +102,14 @@
         near_ref[:, chunk_of(c)] = own[c, :tokens] + recv[c, :tokens]
         total = own[c, tokens:] + recv[c, tokens:]
 
-        @pl.when(c < EARLY)
-        def _():
-            early_src[0] = total
-
-        @pl.when(c >= EARLY)
-        def _():
-            far_ref[:, chunk_of(c - EARLY)] = total
+        @pl.when(c == 0)
+        def _():
+            early_src[...] = total[:, :EARLY]
+            far_ref[:, :CHUNK - EARLY] = total[:, EARLY:]
+
+        @pl.when(c >= 1)
+        def _():
+            far_ref[:, pl.ds(pl.multiple_of(c * CHUNK - EARLY, 128), CHUNK)] = total
 
     def step(c, carry):
         fetch_w(c).wait()
@@ -123,7 +135,7 @@
 
         @pl.when(c == 2)
         def _():
-            early(0).start()
+            early.start()
 
         return carry
 
@@ -134,8 +146,7 @@
     fetch_x.wait()
     for c in range(chunks):
         to_sibling(c).wait_send()
-    for c in range(EARLY):
-        early(c).wait()
+    early.wait()
     for p in range(PIECES):
         cross_piece(p).wait_send()
         last_piece(p).wait()
@@ -150,8 +161,8 @@
         front_kernel,
         out_shape=(
             jax.ShapeDtypeStruct((tokens, hidden), jnp.float32),
-            jax.ShapeDtypeStruct((tokens, hidden - EARLY * CHUNK), jnp.float32),
-            jax.ShapeDtypeStruct((EARLY, tokens, CHUNK), jnp.float32),
+            jax.ShapeDtypeStruct((tokens, hidden - EARLY), jnp.float32),
+            jax.ShapeDtypeStruct((tokens, EARLY), jnp.float32),
             jax.ShapeDtypeStruct((4 * tokens, hidden), x.dtype),
             jax.ShapeDtypeStruct(g.shape, g.dtype),
         ),
@@ -160,9 +171,9 @@
         scratch_shapes=[
             pltpu.VMEM((SLOTS, CHUNK, ffn), w.dtype),
             sums, sums, sums,
-            pltpu.VMEM((EARLY, tokens, CHUNK), jnp.float32),
+            pltpu.VMEM((tokens, EARLY), jnp.float32),
             dma, dma((4,)), dma((SLOTS,)), dma((chunks,)), dma((chunks,)), dma, dma,
-            dma((PIECES,)), dma((PIECES,)), dma((PIECES,)), dma((PIECES,)), dma((EARLY,)), dma((EARLY,)),
+            dma((PIECES,)), dma((PIECES,)), dma((PIECES,)), dma((PIECES,)), dma, dma,
         ],
         cost_estimate=pl.CostEstimate(
             flops=2 * g.shape[0] * hidden * ffn, bytes_accessed=2 * hidden * ffn, transcendentals=0),
@@ -221,7 +232,7 @@
         near, far, early, x_all, g_all = front(x, g, w)
         arrived = lax.ppermute(far, "tp", CROSS)
         grad_w = dw(x_all, g_all)
-        arrived = jnp.concatenate([early[c] for c in range(EARLY)] + [arrived], axis=1)
+        arrived = jnp.concatenate([early, arrived], axis=1)
         return (near + arrived).astype(jnp.bfloat16), grad_w
 
     return jax.shard_map(

time: 44.8 us -> 44.7 us (level)
  Pallas kernels: 41.1 us -> 39.1 us
  starting transfers between devices: 0.58 us -> 2.16 us
    pallas_call x1, Pallas kernels: 19.5 us -> 17.6 us  [front(): pl.pallas_call(front_kernel, out_shape=(jax.ShapeDtypeStruct((tokens, hid...]
    ppermute x1, starting transfers between devices: 0.58 us -> 2.16 us  [per_device(): arrived = lax.ppermute(far, 'tp', CROSS)]
where the time goes in v5:
time: 44.7 us; the launch traced here: 44.6 us
  Pallas kernels  39.1 us (87%)
  starting transfers between devices  2.16 us (5%)
  local copies, waits for them, and re-layouts  1.03 us (2%)
  other arithmetic  0.89 us (2%)
  waiting for transfers between devices  0.68 us (2%)
  between operations  0.66 us (1%)
    pallas_call x1, Pallas kernels, dw(): pl.pallas_call(dw_kernel, out_shape=jax.ShapeDtypeStruct((hidden, ffn), j...  21.5 us
    pallas_call x1, Pallas kernels, front(): pl.pallas_call(front_kernel, out_shape=(jax.ShapeDtypeStruct((tokens, hid...  17.6 us
    ppermute x1, starting transfers between devices, per_device(): arrived = lax.ppermute(far, 'tp', CROSS)  2.16 us
    unnamed x2, local copies, waits for them, and re-layouts  1.03 us
  transfers between devices with their start and end apart: 1, of which 1 were waited for; matrix products, arithmetic and copies ran while one was open for 0% of the time, Pallas kernels for 48%

profile of v5, /device:TPU:0, one launch (start us, length us, event | category | flops | bytes accessed | tf_op | source)
XLA Modules:
  0.0 44.6 jit_solution(556791215205677055)
XLA Ops:
  0.6 0.0 copy-start
  0.6 1.0 %copy-done = bf16[64,4096]{1,0:T(8,128)(2,1)S(1)} copy-done((bf16[64,4096]{1,0:T(8,128)(2,1)S(1)}, bf16[64,4096]{1,0:T(8,128)(2,1)}, u32[]{:S(2)}) %copy-start) | copy-done | bytes 524312
  1.7 17.6 %front.1 = (f32[64,4096]{1,0:T(8,128)S(1)}, f32[64,3840]{1,0:T(8,128)S(1)}, f32[64,256]{1,0:T(8,128)S(1)}, bf16[256,4096]{1,0:T(8,128)(2,1)S(1)}, bf16[256,4096]{1,0:T(8,128)(2,1)S(1)}) custom-call(bf16[64,4096]{1,0:T(8,128)(2,1)S(1)} %copy-done, bf16[256,4096]{1,0:T(8,128)(2,1)} %g_ref.1, bf16[4096,4096]{1,0:T(8,128)(2,1)} %w_ref.1), custom_call_target="tpu_custom_call" | custom-call | flops 8589934592 | bytes 33554432 | tf_op jit(solution)/shard_map/front/pallas_call | solution.py:160
  19.3 2.2 %collective-permute-start = (f32[64,3840]{1,0:T(8,128)S(1)}, f32[64,3840]{1,0:T(8,128)S(1)}, u32[]{:S(2)}, u32[]{:S(2)}) collective-permute-start(f32[64,3840]{1,0:T(8,128)S(1)} %get-tuple-element.9), channel_id=1, source_target_pairs={{0,2},{1,3},{2,0},{3,1},{4,6},{5,7},{6,4},{7,5},{8,10},{9,11},{10,... | collective-permute-start | bytes 2949128 | tf_op jit(solution)/shard_map/ppermute | solution.py:233
  21.5 21.5 %dw.1 = f32[4096,4096]{1,0:T(8,128)} custom-call(bf16[256,4096]{1,0:T(8,128)(2,1)S(1)} %get-tuple-element.10.x_ref, bf16[256,4096]{1,0:T(8,128)(2,1)S(1)} %get-tuple-element.11.g_ref), custom_call_target="tpu_custom_call" | custom-call | flops 8589934592 | bytes 67108864 | tf_op jit(solution)/shard_map/dw/pallas_call | solution.py:214
  43.0 0.7 %collective-permute-done = f32[64,3840]{1,0:T(8,128)S(1)} collective-permute-done((f32[64,3840]{1,0:T(8,128)S(1)}, f32[64,3840]{1,0:T(8,128)S(1)}, u32[]{:S(2)}, u32[]{:S(2)}) %collective-permute-start) | collective-permute-done | bytes 983072 | tf_op jit(solution)/shard_map/ppermute | solution.py:233
  43.7 0.9 %fusion = bf16[64,4096]{1,0:T(8,128)(2,1)} fusion(f32[64,4096]{1,0:T(8,128)S(1)} %get-tuple-element.7, f32[64,3840]{1,0:T(8,128)S(1)} %collective-permute-done, f32[64,256]{1,0:T(8,128)S(1)} %get-tuple-element.8), kind=kLoop, calls=%fused_computation.1 | loop fusion | flops 786432 | bytes 2621440 | tf_op jit(solution)/shard_map/convert_element_type | solution.py:236
Async XLA Ops:
  0.6 1.0 %copy-start = (bf16[64,4096]{1,0:T(8,128)(2,1)S(1)}, bf16[64,4096]{1,0:T(8,128)(2,1)}, u32[]{:S(2)}) copy-start(bf16[64,4096]{1,0:T(8,128)(2,1)} %x_ref.1) | copy-start | bytes 1572868
  19.3 24.4 %collective-permute-start = (f32[64,3840]{1,0:T(8,128)S(1)}, f32[64,3840]{1,0:T(8,128)S(1)}, u32[]{:S(2)}, u32[]{:S(2)}) collective-permute-start(f32[64,3840]{1,0:T(8,128)S(1)} %get-tuple-element.9), channel_id=1, source_target_pairs={{0,2},{1,3},{2,0},{3,1},{4,6},{5,7},{6,4},{7,5},{8,10},{9,11},{10,... | collective-permute-start | bytes 2949128 | tf_op jit(solution)/shard_map/ppermute | solution.py:233

commit v6 on v5

--- a/solution.py
+++ b/solution.py
@@ -128,8 +128,8 @@
             finish(c - 1)
 
         to_sibling(c).start()
-        for p in range(PIECES - 1):
-            @pl.when(c == 2 * p + 2)
+        for p, when in enumerate((2, 4, 6, 7)):
+            @pl.when(c == when)
             def _():
                 forward(p)
 
@@ -141,7 +141,6 @@
 
     lax.fori_loop(0, chunks, step, 0)
     finish(chunks - 1)
-    forward(PIECES - 1)
     x_to_sibling.wait()
     fetch_x.wait()
     for c in range(chunks):
@@ -229,6 +228,7 @@
 
 def solution(mesh):
     def per_device(x, w, g):
+        x = pltpu.with_memory_space_constraint(x, pltpu.HBM)
         near, far, early, x_all, g_all = front(x, g, w)
         arrived = lax.ppermute(far, "tp", CROSS)
         grad_w = dw(x_all, g_all)

time: 44.7 us -> 43.3 us (0.969)
  local copies, waits for them, and re-layouts: 1.03 us -> 0 us
  starting transfers between devices: 2.16 us -> 1.38 us
    unnamed x2 -> x0, local copies, waits for them, and re-layouts: 1.03 us -> none
    ppermute x1, starting transfers between devices: 2.16 us -> 1.38 us  [per_device(): arrived = lax.ppermute(far, 'tp', CROSS)]
  transfers between devices with their start and end apart: 1 -> 1, of which waited for: 1 -> 1; matrix products, arithmetic and copies ran while one was open for 0% -> 0% of each run, Pallas kernels for 48% -> 50%
where the time goes in v6:
time: 43.3 us; the launch traced here: 43.2 us
  Pallas kernels  39.4 us (91%)
  starting transfers between devices  1.38 us (3%)
  waiting for transfers between devices  0.9 us (2%)
  other arithmetic  0.89 us (2%)
  between operations  0.65 us (2%)
    pallas_call x1, Pallas kernels, dw(): pl.pallas_call(dw_kernel, out_shape=jax.ShapeDtypeStruct((hidden, ffn), j...  21.5 us
    pallas_call x1, Pallas kernels, front(): pl.pallas_call(front_kernel, out_shape=(jax.ShapeDtypeStruct((tokens, hid...  17.8 us
    ppermute x1, starting transfers between devices, per_device(): arrived = lax.ppermute(far, 'tp', CROSS)  1.38 us
    ppermute x1, waiting for transfers between devices, per_device(): arrived = lax.ppermute(far, 'tp', CROSS)  0.9 us
    convert_element_type x1, other arithmetic, per_device(): return ((near + arrived).astype(jnp.bfloat16), grad_w)  0.89 us
  transfers between devices with their start and end apart: 1, of which 1 were waited for; matrix products, arithmetic and copies ran while one was open for 0% of the time, Pallas kernels for 50%

profile of v6, /device:TPU:0, one launch (start us, length us, event | category | flops | bytes accessed | tf_op | source)
XLA Modules:
  0.0 43.2 jit_solution(9814419461734427131)
XLA Ops:
  0.6 17.8 %front.1 = (f32[64,4096]{1,0:T(8,128)S(1)}, f32[64,3840]{1,0:T(8,128)S(1)}, f32[64,256]{1,0:T(8,128)S(1)}, bf16[256,4096]{1,0:T(8,128)(2,1)S(1)}, bf16[256,4096]{1,0:T(8,128)(2,1)S(1)}) custom-call(bf16[64,4096]{1,0:T(8,128)(2,1)} %x_ref.1, bf16[256,4096]{1,0:T(8,128)(2,1)} %g_ref.1, bf16[4096,4096]{1,0:T(8,128)(2,1)} %w_ref.1), custom_call_target="tpu_custom_call" | custom-call | flops 8589934592 | bytes 33554432 | tf_op jit(solution)/shard_map/front/pallas_call | solution.py:159
  18.5 1.4 %collective-permute-start = (f32[64,3840]{1,0:T(8,128)S(1)}, f32[64,3840]{1,0:T(8,128)S(1)}, u32[]{:S(2)}, u32[]{:S(2)}) collective-permute-start(f32[64,3840]{1,0:T(8,128)S(1)} %get-tuple-element.9), channel_id=1, source_target_pairs={{0,2},{1,3},{2,0},{3,1},{4,6},{5,7},{6,4},{7,5},{8,10},{9,11},{10,... | collective-permute-start | bytes 2949128 | tf_op jit(solution)/shard_map/ppermute | solution.py:233
  19.9 21.5 %dw.1 = f32[4096,4096]{1,0:T(8,128)} custom-call(bf16[256,4096]{1,0:T(8,128)(2,1)S(1)} %get-tuple-element.10.x_ref, bf16[256,4096]{1,0:T(8,128)(2,1)S(1)} %get-tuple-element.11.g_ref), custom_call_target="tpu_custom_call" | custom-call | flops 8589934592 | bytes 67108864 | tf_op jit(solution)/shard_map/dw/pallas_call | solution.py:213
  41.4 0.9 %collective-permute-done = f32[64,3840]{1,0:T(8,128)S(1)} collective-permute-done((f32[64,3840]{1,0:T(8,128)S(1)}, f32[64,3840]{1,0:T(8,128)S(1)}, u32[]{:S(2)}, u32[]{:S(2)}) %collective-permute-start) | collective-permute-done | bytes 983072 | tf_op jit(solution)/shard_map/ppermute | solution.py:233
  42.3 0.9 %fusion = bf16[64,4096]{1,0:T(8,128)(2,1)} fusion(f32[64,4096]{1,0:T(8,128)S(1)} %get-tuple-element.7, f32[64,3840]{1,0:T(8,128)S(1)} %collective-permute-done, f32[64,256]{1,0:T(8,128)S(1)} %get-tuple-element.8), kind=kLoop, calls=%fused_computation.1 | loop fusion | flops 786432 | bytes 2621440 | tf_op jit(solution)/shard_map/convert_element_type | solution.py:236
Async XLA Ops:
  18.5 23.8 %collective-permute-start = (f32[64,3840]{1,0:T(8,128)S(1)}, f32[64,3840]{1,0:T(8,128)S(1)}, u32[]{:S(2)}, u32[]{:S(2)}) collective-permute-start(f32[64,3840]{1,0:T(8,128)S(1)} %get-tuple-element.9), channel_id=1, source_target_pairs={{0,2},{1,3},{2,0},{3,1},{4,6},{5,7},{6,4},{7,5},{8,10},{9,11},{10,... | collective-permute-start | bytes 2949128 | tf_op jit(solution)/shard_map/ppermute | solution.py:233
